TPU v7x, 256 devices: a whole 4x4x8 slice. The times are simulated.
256 devices in a mesh: dp: 32 (over x, z), mp: 8 (over y, core).
Axes of the slice: x: 4, y: 4, z: 8, core: 2. Of those that a mesh axis runs over, the one named last changes fastest.
Arguments:
- query_emb: bfloat16 [8192, 768], P('dp'), may hold values from -6 to 6
- positive_list: int32 [8192], replicated, may hold values from 0 to 32767
- centroids: float32 [32768, 768], P(('dp', 'mp')), may hold values from -0.6 to 0.6
- first_moment: float32 [32768, 768], P(('dp', 'mp')), may hold values from -3 to 3
- second_moment: float32 [32768, 768], P(('dp', 'mp')), may hold values from 0.05 to 2
Outputs:
- new_centroids: float32 [32768, 768], P(('dp', 'mp'))
- new_first: float32 [32768, 768], P(('dp', 'mp'))
- new_second: float32 [32768, 768], P(('dp', 'mp'))
- mean_loss: float32 [], replicated
All inputs are finite; a program needn't handle non-finite values.
Results may differ from a plain program's by a relative error of at most 0.00097.
Values may be sent and summed in bfloat16 or wider, within the bound.
No kernel may reach another device: no remote copies, remote signals or barrier semaphores. Data moves between devices by JAX's collectives and lax.ppermute only.
A program may use at most 64 MiB of HBM per device.

v0:
```python
import jax
import jax.numpy as jnp
from jax import lax
from jax.sharding import Mesh
from jax.sharding import PartitionSpec as P

MP = ("mp_0", "mp_1")
DP = ("dp_0", "dp_1")
DP_MP = ("dp_0", "dp_1", "mp_0", "mp_1")
beta_first = 0.9
beta_second = 0.95
learn_rate = 0.01
epsilon = 1e-08


def all_in_one(x, axis):
    leaves = jax.tree.leaves(x)
    turns = sorted(range(len(leaves)), key=lambda k: -leaves[k].size)
    width = (1, *leaves[turns[0]].shape)[-1]
    lines = [
        jnp.pad(leaves[k].reshape(-1), (0, -leaves[k].size % width)).reshape(-1, width)
        for k in turns
    ]
    both, at, found = (lax.all_gather(jnp.concatenate(lines), axis), 0, {})
    for k, line in zip(turns, lines):
        piece = both[:, at : at + len(line)].reshape(len(both), -1)
        found[k] = piece[:, : leaves[k].size].reshape(-1, *leaves[k].shape)
        at += len(line)
    numbers = iter(range(len(leaves)))
    return jax.tree.map(lambda _: found[next(numbers)], x)


def combined_by_axis(x, axes, combine):
    for axis in axes:
        pieces = all_in_one(x, axis)
        x = jax.tree.map(lambda part: part[0], pieces)
        for k in range(1, lax.axis_size(axis)):
            x = combine(x, jax.tree.map(lambda part: part[k], pieces))
    return x


def adam_update(centroids, first_moment, second_moment, gradient):
    new_first = beta_first * first_moment + (1.0 - beta_first) * gradient
    new_second = beta_second * second_moment + (1.0 - beta_second) * gradient * gradient
    new_centroids = centroids - learn_rate * new_first / (jnp.sqrt(new_second) + epsilon)
    return (new_centroids, new_first, new_second)


def combine(left_part, right_part):
    top_value = jnp.maximum(left_part[0], right_part[0])
    summed = left_part[1] * jnp.exp(left_part[0] - top_value) + right_part[1] * jnp.exp(
        right_part[0] - top_value
    )
    return (top_value, summed, left_part[2] + right_part[2])


def target_logit(logits, is_target):
    return jnp.sum(jnp.where(is_target, logits, jnp.zeros_like(logits)), axis=1)


def row_terms(logits, is_target, row_peak, row_mass, row_target):
    log_norm = row_peak + jnp.log(row_mass)
    row_loss = log_norm - row_target
    weights = (jnp.exp(logits - log_norm[:, None]) - is_target.astype(jnp.float32)).astype(
        jnp.bfloat16
    )
    return (row_loss, weights)


def shards(query_emb, positive_list, centroids, first_moment, second_moment):
    table_half = centroids.astype(jnp.bfloat16)
    own_lists = centroids.shape[0]
    count_mp = lax.axis_size(MP)
    dp_index = lax.axis_index(DP)
    mp_index = lax.axis_index(MP)
    gathered = lax.all_gather(query_emb, DP, axis=0, tiled=True)
    logits = jnp.einsum("rd,kd->rk", gathered, table_half, preferred_element_type=jnp.float32)
    shard_block = dp_index * count_mp + mp_index
    global_col = shard_block * own_lists + lax.iota(jnp.int32, own_lists)
    is_target = global_col[None, :] == positive_list[:, None]
    local_peak = jnp.max(logits, axis=1)
    local_mass = jnp.sum(jnp.exp(logits - local_peak[:, None]), axis=1)
    row_peak, row_mass, row_target = combined_by_axis(
        (local_peak, local_mass, target_logit(logits, is_target)), DP_MP, combine
    )
    row_loss, weights = row_terms(logits, is_target, row_peak, row_mass, row_target)
    mean_loss = jnp.mean(row_loss)
    gradient = jnp.einsum("rk,rd->kd", weights, gathered, preferred_element_type=jnp.float32)
    new_centroids, new_first, new_second = adam_update(
        centroids, first_moment, second_moment, gradient
    )
    return (new_centroids, new_first, new_second, mean_loss)


def solution(mesh):
    split = Mesh(mesh.devices.reshape(4, 8, 4, 2), ("dp_0", "dp_1", "mp_0", "mp_1"))
    placed = (P(DP, None), P(), P(DP_MP, None), P(DP_MP, None), P(DP_MP, None))
    return jax.shard_map(
        shards,
        mesh=split,
        in_specs=placed,
        out_specs=(P(DP_MP, None), P(DP_MP, None), P(DP_MP, None), P()),
        check_vma=False,
    )
```

profile of v0, /device:TPU:1, one launch (start us, length us, event | category | flops | bytes accessed | tf_op | source)
XLA Modules:
  0.0 219.7 jit_solution(9997302614362853183)
XLA Ops:
  7.2 0.0 all-gather.10.cloned.1.call-start
  7.2 0.7 all-gather.10.cloned.1.call-update
  7.9 0.0 copy-start.4
  7.9 124.4 %all-gather.10.cloned.1.call-done = bf16[8192,768]{1,0:T(8,128)(2,1)} async-done(((bf16[256,768]{1,0:T(8,128)(2,1)}), bf16[8192,768]{1,0:T(8,128)(2,1)}) %all-gather.10.cloned.1.call-update) | async-done | bytes 12582928 | tf_op jit(solution)/shard_map/all_gather | solution.py:76
  132.3 8.7 %fusion.73 = (f32[8192]{0:T(1024)S(1)}, f32[8192,128]{0,1:T(8,128)S(1)}) fusion(bf16[8192,768]{1,0:T(8,128)(2,1)} %all-gather.10.cloned.1.call-done, f32[128,768]{1,0:T(8,128)} %param.7), kind=kOutput, calls=%fused_computation.128 | convolution fusion | flops 1611751424 | bytes 17203200 | tf_op jit(solution)/shard_map/rd,kd->rk/dot_general | solution.py:77
  141.0 0.0 copy-start
  141.0 0.0 copy-done.4
  141.1 1.1 exponential_reduce_fusion
  142.1 0.0 copy-start.1
  142.1 0.0 copy-start.2
  142.1 0.0 copy-start.3
  142.2 0.1 maximum_bitcast_fusion
  142.3 10.2 %all-gather.4 = f32[4,3,8192]{2,1,0:T(4,128)S(1)} all-gather(f32[1,3,8192]{2,1,0:T(4,128)S(1)} %maximum_bitcast_fusion), channel_id=2, replica_groups=mesh['dp_0'=4,'dp_1'=8,'mp_0'=4,'mp_1'=2] {'dp_0'}, dimensions={0}, use_global_device_ids=true | all-gather | bytes 491520 | tf_op jit(solution)/shard_map/all_gather | solution.py:24
  152.5 0.1 fusion.43
  152.6 0.3 fusion.45
  153.0 0.1 maximum_bitcast_fusion.1
  153.1 21.0 %all-gather.5 = f32[8,3,8192]{2,1,0:T(4,128)S(1)} all-gather(f32[1,3,8192]{2,1,0:T(4,128)S(1)} %maximum_bitcast_fusion.1), channel_id=3, replica_groups=mesh['dp_0'=4,'dp_1'=8,'mp_0'=4,'mp_1'=2] {'dp_1'}, dimensions={0}, use_global_device_ids=true | all-gather | bytes 884736 | tf_op jit(solution)/shard_map/all_gather | solution.py:24
  174.0 0.2 fusion.21
  174.2 0.7 fusion.23
  175.0 0.1 maximum_bitcast_fusion.2
  175.1 10.5 %all-gather.6 = f32[4,3,8192]{2,1,0:T(4,128)S(1)} all-gather(f32[1,3,8192]{2,1,0:T(4,128)S(1)} %maximum_bitcast_fusion.2), channel_id=4, replica_groups=mesh['dp_0'=4,'dp_1'=8,'mp_0'=4,'mp_1'=2] {'mp_0'}, dimensions={0}, use_global_device_ids=true | all-gather | bytes 491520 | tf_op jit(solution)/shard_map/all_gather | solution.py:24
  185.6 0.0 copy-done
  185.6 0.1 fusion.11
  185.7 0.3 fusion.13
  186.1 0.1 maximum_bitcast_fusion.3
  186.2 14.9 %all-gather.7 = f32[2,3,8192]{2,1,0:T(4,128)S(1)} all-gather(f32[1,3,8192]{2,1,0:T(4,128)S(1)} %maximum_bitcast_fusion.3), channel_id=5, replica_groups=mesh['dp_0'=4,'dp_1'=8,'mp_0'=4,'mp_1'=2] {'mp_1'}, dimensions={0}, use_global_device_ids=true | all-gather | bytes 294912 | tf_op jit(solution)/shard_map/all_gather | solution.py:24
  201.1 0.1 fusion.72
  201.2 0.6 subtract_reduce_fusion
  202.5 0.0 copy-done.1
  202.5 0.0 copy-done.2
  202.5 0.0 copy-done.3
  202.5 9.2 %divide_subtract_fusion = (f32[128,768]{1,0:T(8,128)}, f32[128,768]{1,0:T(8,128)}, f32[128,768]{1,0:T(8,128)}) fusion(f32[128,768]{1,0:T(8,128)S(1)} %copy-done.1, f32[128,768]{1,0:T(8,128)S(1)} %copy-done.2, f32[128,768]{1,0:T(8,128)S(1)} %copy-done.3, bf16[8192,768]{1,0:T(8,128)(2,1)} %all-gather.10.cloned.1.call-done, f32[8192,128]{0,1:T(8,128)} %copy-done, ...), kind=kOutput, calls=%fused_computation.12 | convolution fusion | flops 1616936960 | bytes 19202560 | tf_op jit(solution)/shard_map/rk,rd->kd/dot_general | solution.py:88
  (1 shorter events, 0.0 us)
Async XLA Ops:
  7.2 125.2 %all-gather.10.cloned.1.call-start = ((), (), s32[]{:S(2)}) async-start(), calls=%async_computation | async-start | bytes 12976128 | tf_op jit(solution)/shard_map/all_gather | solution.py:76
  7.9 133.1 %copy-start.4 = (s32[8192]{0:T(1024)S(1)}, s32[8192]{0:T(1024)}, u32[]{:S(2)}) copy-start(s32[8192]{0:T(1024)} %param.6) | copy-start | bytes 98308
  141.0 44.6 %copy-start = (f32[8192,128]{0,1:T(8,128)}, f32[8192,128]{0,1:T(8,128)S(1)}, u32[]{:S(2)}) copy-start(f32[8192,128]{0,1:T(8,128)S(1)} %get-tuple-element.23) | copy-start | bytes 12582916
  142.1 60.4 %copy-start.1 = (f32[128,768]{1,0:T(8,128)S(1)}, f32[128,768]{1,0:T(8,128)}, u32[]{:S(2)}) copy-start(f32[128,768]{1,0:T(8,128)} %param.7) | copy-start | bytes 1179652
  142.1 60.4 %copy-start.2 = (f32[128,768]{1,0:T(8,128)S(1)}, f32[128,768]{1,0:T(8,128)}, u32[]{:S(2)}) copy-start(f32[128,768]{1,0:T(8,128)} %param.8) | copy-start | bytes 1179652
  142.1 60.4 %copy-start.3 = (f32[128,768]{1,0:T(8,128)S(1)}, f32[128,768]{1,0:T(8,128)}, u32[]{:S(2)}) copy-start(f32[128,768]{1,0:T(8,128)} %param.9) | copy-start | bytes 1179652
Sparse Core Ops, SparseCore 0:
  10.6 121.7 all-gather.9
where the time goes:
time: 220 us
  waiting for transfers between devices  125 us (57%)
  blocking collectives  56.6 us (26%)
  matrix products  17.9 us (8%)
  between operations  16 us (7%)
  other arithmetic  4.04 us (2%)
    all_gather x1, waiting for transfers between devices, shards(): gathered = lax.all_gather(query_emb, DP, axis=0, tiled=True)  124 us
    all_gather x4, blocking collectives, all_in_one(): both, at, found = (lax.all_gather(jnp.concatenate(lines), axis), 0, {})  56.6 us
    dot_general x1, matrix products, shards(): jnp.einsum('rk,rd->kd', weights, gathered, preferred_element_type=jnp.flo...  9.24 us
    dot_general x1, matrix products, shards(): jnp.einsum('rd,kd->rk', gathered, table_half, preferred_element_type=jnp....  8.7 us
  transfers between devices with their start and end apart: 1, of which 1 were waited for; matrix products, arithmetic and copies ran while one was open for 0% of the time, Pallas kernels for 0%

commit v1 on v0

--- a/solution.py
+++ b/solution.py
@@ -73,7 +73,9 @@
     count_mp = lax.axis_size(MP)
     dp_index = lax.axis_index(DP)
     mp_index = lax.axis_index(MP)
-    gathered = lax.all_gather(query_emb, DP, axis=0, tiled=True)
+    gathered = jnp.concatenate(
+        lax.all_to_all(jnp.stack([query_emb] * lax.axis_size(DP)), DP, 0, 0), axis=0
+    )
     logits = jnp.einsum("rd,kd->rk", gathered, table_half, preferred_element_type=jnp.float32)
     shard_block = dp_index * count_mp + mp_index
     global_col = shard_block * own_lists + lax.iota(jnp.int32, own_lists)

time: 220 us -> 397 us (1.80)
  waiting for transfers between devices: 125 us -> 280 us
  blocking collectives: 56.6 us -> 72.6 us
  between operations: 16 us -> 2.56 us
  starting transfers between devices: 0.04 us -> 12.1 us
  local copies, waits for them, and re-layouts: 0.03 us -> 6.91 us
    all_to_all x0 -> x1, waiting for transfers between devices: none -> 280 us  [shards(): lax.all_to_all(jnp.stack([query_emb] * lax.axis_size(DP)), DP, 0, 0)]
    all_gather x1 -> x0, waiting for transfers between devices: 124 us -> none  [shards(): gathered = lax.all_gather(query_emb, DP, axis=0, tiled=True)]
    all_gather x4, blocking collectives: 56.6 us -> 72.6 us  [all_in_one(): both, at, found = (lax.all_gather(jnp.concatenate(lines), axis), 0, {})]
    all_to_all x0 -> x1, starting transfers between devices: none -> 12.1 us  [shards(): lax.all_to_all(jnp.stack([query_emb] * lax.axis_size(DP)), DP, 0, 0)]
    another operation x0 -> x1, local copies, waits for them, and re-layouts: none -> 6.89 us  [shards(): jnp.stack([query_emb] * lax.axis_size(DP))]
where the time goes in v1:
time: 397 us
  waiting for transfers between devices  280 us (71%)
  blocking collectives  72.6 us (18%)
  matrix products  17.9 us (5%)
  starting transfers between devices  12.1 us (3%)
  local copies, waits for them, and re-layouts  6.91 us (2%)
  other arithmetic  4.04 us (1%)
    all_to_all x1, waiting for transfers between devices, shards(): lax.all_to_all(jnp.stack([query_emb] * lax.axis_size(DP)), DP, 0, 0)  280 us
    all_gather x4, blocking collectives, all_in_one(): both, at, found = (lax.all_gather(jnp.concatenate(lines), axis), 0, {})  72.6 us
    all_to_all x1, starting transfers between devices, shards(): lax.all_to_all(jnp.stack([query_emb] * lax.axis_size(DP)), DP, 0, 0)  12.1 us
    dot_general x1, matrix products, shards(): jnp.einsum('rk,rd->kd', weights, gathered, preferred_element_type=jnp.flo...  9.23 us
    dot_general x1, matrix products, shards(): jnp.einsum('rd,kd->rk', gathered, table_half, preferred_element_type=jnp....  8.72 us
  transfers between devices with their start and end apart: 1, of which 1 were waited for; matrix products, arithmetic and copies ran while one was open for 0% of the time, Pallas kernels for 0%

profile of v1, /device:TPU:1, one launch (start us, length us, event | category | flops | bytes accessed | tf_op | source)
XLA Modules:
  0.0 396.7 jit_solution(9850300474844215375)
XLA Ops:
  0.6 6.9 %stack.2 = bf16[32,256,768]{2,1,0:T(8,128)(2,1)} broadcast(bf16[256,768]{1,0:T(8,128)(2,1)} %param.5), dimensions={1,2} | broadcast | bytes 12976128 | tf_op jit(solution)/shard_map/stack | solution.py:77
  7.5 0.0 copy-start.1
  7.5 12.1 %all-to-all-start = ((bf16[32,256,768]{2,1,0:T(8,128)(2,1)}), bf16[32,256,768]{2,1,0:T(8,128)(2,1)}, u32[]{:S(2)}, u32[]{:S(2)}) async-start(bf16[32,256,768]{2,1,0:T(8,128)(2,1)} %stack.2), calls=%async_computation | async-start | bytes 25165824 | tf_op jit(solution)/shard_map/all_to_all | solution.py:77
  19.6 280.5 %all-to-all-done = bf16[32,256,768]{2,1,0:T(8,128)(2,1)} async-done(((bf16[32,256,768]{2,1,0:T(8,128)(2,1)}), bf16[32,256,768]{2,1,0:T(8,128)(2,1)}, u32[]{:S(2)}, u32[]{:S(2)}) %all-to-all-start) | async-done | bytes 12582944 | tf_op jit(solution)/shard_map/all_to_all | solution.py:77
  300.1 0.0 copy-done.1
  300.1 0.0 copy-start.4
  300.1 8.7 %fusion.73 = (f32[8192]{0:T(1024)S(1)}, f32[8192,128]{0,1:T(8,128)S(1)}) fusion(bf16[8192,768]{1,0:T(8,128)(2,1)} %bitcast, f32[128,768]{1,0:T(8,128)S(1)} %copy-done.1), kind=kOutput, calls=%fused_computation.128 | convolution fusion | flops 1611751424 | bytes 17203200 | tf_op jit(solution)/shard_map/rd,kd->rk/dot_general | solution.py:79
  308.9 0.0 copy-start
  308.9 0.0 copy-done.4
  308.9 1.1 exponential_reduce_fusion
  309.9 0.0 copy-start.2
  310.0 0.0 copy-start.3
  310.0 0.1 maximum_bitcast_fusion
  310.1 22.0 %all-gather.4 = f32[4,3,8192]{2,1,0:T(4,128)S(1)} all-gather(f32[1,3,8192]{2,1,0:T(4,128)S(1)} %maximum_bitcast_fusion), channel_id=2, replica_groups=mesh['dp_0'=4,'dp_1'=8,'mp_0'=4,'mp_1'=2] {'dp_0'}, dimensions={0}, use_global_device_ids=true | all-gather | bytes 491520 | tf_op jit(solution)/shard_map/all_gather | solution.py:24
  332.1 0.1 fusion.43
  332.2 0.3 fusion.45
  332.5 0.1 maximum_bitcast_fusion.1
  332.6 28.6 %all-gather.5 = f32[8,3,8192]{2,1,0:T(4,128)S(1)} all-gather(f32[1,3,8192]{2,1,0:T(4,128)S(1)} %maximum_bitcast_fusion.1), channel_id=3, replica_groups=mesh['dp_0'=4,'dp_1'=8,'mp_0'=4,'mp_1'=2] {'dp_1'}, dimensions={0}, use_global_device_ids=true | all-gather | bytes 884736 | tf_op jit(solution)/shard_map/all_gather | solution.py:24
  361.2 0.2 fusion.21
  361.4 0.7 fusion.23
  362.2 0.1 maximum_bitcast_fusion.2
  362.3 10.7 %all-gather.6 = f32[4,3,8192]{2,1,0:T(4,128)S(1)} all-gather(f32[1,3,8192]{2,1,0:T(4,128)S(1)} %maximum_bitcast_fusion.2), channel_id=4, replica_groups=mesh['dp_0'=4,'dp_1'=8,'mp_0'=4,'mp_1'=2] {'mp_0'}, dimensions={0}, use_global_device_ids=true | all-gather | bytes 491520 | tf_op jit(solution)/shard_map/all_gather | solution.py:24
  373.0 0.0 copy-done
  373.0 0.1 fusion.11
  373.1 0.3 fusion.13
  373.4 0.1 maximum_bitcast_fusion.3
  373.5 11.3 %all-gather.7 = f32[2,3,8192]{2,1,0:T(4,128)S(1)} all-gather(f32[1,3,8192]{2,1,0:T(4,128)S(1)} %maximum_bitcast_fusion.3), channel_id=5, replica_groups=mesh['dp_0'=4,'dp_1'=8,'mp_0'=4,'mp_1'=2] {'mp_1'}, dimensions={0}, use_global_device_ids=true | all-gather | bytes 294912 | tf_op jit(solution)/shard_map/all_gather | solution.py:24
  384.9 0.1 fusion.72
  385.0 0.6 subtract_reduce_fusion
  386.3 0.0 copy-done.2
  386.3 0.0 copy-done.3
  386.3 9.2 %divide_subtract_fusion = (f32[128,768]{1,0:T(8,128)}, f32[128,768]{1,0:T(8,128)}, f32[128,768]{1,0:T(8,128)}) fusion(f32[128,768]{1,0:T(8,128)S(1)} %copy-done.1, f32[128,768]{1,0:T(8,128)S(1)} %copy-done.2, f32[128,768]{1,0:T(8,128)S(1)} %copy-done.3, bf16[8192,768]{1,0:T(8,128)(2,1)} %bitcast, f32[8192,128]{0,1:T(8,128)} %copy-done, ...), kind=kOutput, calls=%fused_computation.12 | convolution fusion | flops 1616936960 | bytes 19202560 | tf_op jit(solution)/shard_map/rk,rd->kd/dot_general | solution.py:90
  (1 shorter events, 0.0 us)
Async XLA Ops:
  7.5 292.6 %copy-start.1 = (f32[128,768]{1,0:T(8,128)S(1)}, f32[128,768]{1,0:T(8,128)}, u32[]{:S(2)}) copy-start(f32[128,768]{1,0:T(8,128)} %param.7) | copy-start | bytes 1179652
  7.5 292.6 %all-to-all-start = ((bf16[32,256,768]{2,1,0:T(8,128)(2,1)}), bf16[32,256,768]{2,1,0:T(8,128)(2,1)}, u32[]{:S(2)}, u32[]{:S(2)}) async-start(bf16[32,256,768]{2,1,0:T(8,128)(2,1)} %stack.2), calls=%async_computation | async-start | bytes 25165824 | tf_op jit(solution)/shard_map/all_to_all | solution.py:77
  300.1 8.7 %copy-start.4 = (s32[8192]{0:T(1024)S(1)}, s32[8192]{0:T(1024)}, u32[]{:S(2)}) copy-start(s32[8192]{0:T(1024)} %param.6) | copy-start | bytes 98308
  308.9 64.1 %copy-start = (f32[8192,128]{0,1:T(8,128)}, f32[8192,128]{0,1:T(8,128)S(1)}, u32[]{:S(2)}) copy-start(f32[8192,128]{0,1:T(8,128)S(1)} %get-tuple-element.23) | copy-start | bytes 12582916
  309.9 76.3 %copy-start.2 = (f32[128,768]{1,0:T(8,128)S(1)}, f32[128,768]{1,0:T(8,128)}, u32[]{:S(2)}) copy-start(f32[128,768]{1,0:T(8,128)} %param.8) | copy-start | bytes 1179652
  310.0 76.3 %copy-start.3 = (f32[128,768]{1,0:T(8,128)S(1)}, f32[128,768]{1,0:T(8,128)}, u32[]{:S(2)}) copy-start(f32[128,768]{1,0:T(8,128)} %param.9) | copy-start | bytes 1179652
